TPU v7x, 128 devices: a whole 4x4x4 slice. The times are simulated.
128 devices in a mesh: dp: 8 (over y_lo, x), tensor: 16 (over y_hi, z, core).
Axes of the slice: x: 4, y: 4 (y_hi: 2, y_lo: 2; y = y_hi * 2 + y_lo), z: 4, core: 2. Of those that a mesh axis runs over, the one named last changes fastest.
Arguments:
- saved_input: bfloat16 [1024, 8192], P(('dp', 'tensor')), may hold values from -8 to 8
- keep_bits: int32 [1024, 448], P(('dp', 'tensor')), may hold values from -2147483648 to 2147483646, as said below
- norm_gain: bfloat16 [8192], P('dp'), may hold values from 0.099609375 to 1.8984375
- gate_weight: bfloat16 [8192, 14336], P('dp', 'tensor'), may hold values from -0.0625 to 0.0625
- up_weight: bfloat16 [8192, 14336], P('dp', 'tensor'), may hold values from -0.0625 to 0.0625
- down_weight: bfloat16 [14336, 8192], P('tensor', 'dp'), may hold values from -0.046875 to 0.046875
Outputs:
- layer_out: bfloat16 [1024, 8192], P('tensor', 'dp')
- row_check: float32 [1024], P('tensor')
Inputs may be any that keep to these rules, and one draw needn't show every extreme that they name: `keep_bits`: bit k of word w of a token is the keep bit of hidden unit 32 w + k.
All inputs are finite; a program needn't handle non-finite values.
Results may differ from a plain program's by a relative error of at most 0.017.
Values may be sent and summed in bfloat16 or wider, within the bound.
No kernel may reach another device: no remote copies, remote signals or barrier semaphores. Data moves between devices by JAX's collectives and lax.ppermute only.
A program may use at most 64 MiB of HBM per device.

v0:
```python
import jax
import jax.numpy as jnp
from jax import lax
from jax.sharding import Mesh
from jax.sharding import PartitionSpec as P

D = 8192
TENSOR = ("tensor_0", "tensor_1", "tensor_2")
DP_TENSOR = ("dp", "tensor_0", "tensor_1", "tensor_2")


def sent_to_all(value, axis):
    length = lax.axis_size(axis)
    return lax.all_to_all(
        jnp.broadcast_to(value[None], (length, *value.shape)), axis, 0, 0, tiled=True
    )


def laid_out(parts, dim):
    lengths = list(parts.shape[1:])
    lengths[dim] *= parts.shape[0]
    return jnp.moveaxis(parts, 0, dim).reshape(lengths)


def whole_of(value, axes, dim):
    far, near = axes
    leading = sent_to_all(value, far)
    parts = jnp.swapaxes(sent_to_all(leading, near), 0, 1)
    return laid_out(parts.reshape(-1, *value.shape), dim)


def over_copies(value, axis):
    everything = sent_to_all(value, axis)
    return jnp.sum(everything, axis=0)


def gathered_copies(value, axis, dim):
    return laid_out(sent_to_all(value, axis), dim)


def in_blocks(value, dim, length):
    before, after = (value.shape[:dim], value.shape[dim + 1 :])
    return jnp.moveaxis(value.reshape(*before, length, -1, *after), dim, 0)


def sum_at_owner(value, axis, dim):
    length = lax.axis_size(axis)
    parts = lax.all_to_all(in_blocks(value, dim, length), axis, 0, 0, tiled=True)
    return jnp.sum(parts.astype(jnp.float32), axis=0)


def sum_in_two_steps(value, axes, dim):
    far, near = axes
    parts = in_blocks(value, dim, lax.axis_size(far))
    nearer = sum_at_owner(parts, near, dim + 1)
    arrived = lax.all_to_all(
        nearer.astype(jnp.bfloat16), far, split_axis=0, concat_axis=0, tiled=True
    )
    return arrived.astype(jnp.float32).sum(axis=0)


def on_device(saved_input, keep_bits, norm_gain, gate_weight, up_weight, down_weight):
    tensor_width = lax.axis_size(TENSOR)
    dp_width = lax.axis_size("dp")
    unit_words = lax.all_to_all(keep_bits, TENSOR, split_axis=1, concat_axis=0, tiled=True)
    shifts = jnp.arange(32, dtype=jnp.int32)
    keep_mask = jnp.bitwise_and(jnp.right_shift(unit_words[:, :, None], shifts[None, None, :]), 1)
    keep_mask = keep_mask.reshape(unit_words.shape[0], -1)
    keep_scale = 2.0 * keep_mask.astype(jnp.float32)
    width_units = gate_weight.shape[1]
    columns = lax.all_to_all(saved_input, "dp", split_axis=1, concat_axis=0, tiled=True)
    collected = whole_of(columns, (("tensor_0", "tensor_1"), "tensor_2"), 0)
    per_device = saved_input.shape[0]
    collected = collected.reshape(tensor_width, dp_width, per_device, collected.shape[1])
    collected = collected.transpose(1, 0, 2, 3).reshape(-1, collected.shape[3])
    widened = collected.astype(jnp.float32)
    squares = over_copies(jnp.sum(widened * widened, axis=1), "dp")
    inv_rms = lax.rsqrt(squares / D + 1e-05)
    normed = (widened * inv_rms[:, None] * norm_gain.astype(jnp.float32)[None, :]).astype(
        jnp.bfloat16
    )
    gate_part = jnp.dot(normed, gate_weight, preferred_element_type=jnp.float32)
    up_part = jnp.dot(normed, up_weight, preferred_element_type=jnp.float32)
    projected = lax.psum_scatter(
        jnp.concatenate((gate_part, up_part), axis=1).astype(jnp.bfloat16),
        "dp",
        scatter_dimension=0,
        tiled=True,
    ).astype(jnp.float32)
    gate_sum = projected[:, :width_units]
    up_sum = projected[:, width_units:]
    hidden = (jax.nn.silu(gate_sum) * up_sum * keep_scale).astype(jnp.bfloat16)
    partial_value = jnp.dot(
        gathered_copies(hidden, "dp", 0), down_weight, preferred_element_type=jnp.float32
    )
    mlp_sum = sum_in_two_steps(
        partial_value.astype(jnp.bfloat16), (("tensor_0", "tensor_1"), "tensor_2"), 0
    )
    out_rows = mlp_sum.shape[0]
    first_row = lax.axis_index(TENSOR) * out_rows
    residual = lax.dynamic_slice_in_dim(collected, first_row, out_rows, 0)
    layer_out = (residual.astype(jnp.float32) + mlp_sum).astype(jnp.bfloat16)
    widened_out = layer_out.astype(jnp.float32)
    row_check = over_copies(jnp.sum(widened_out * widened_out, axis=1), "dp") / D
    return (layer_out, row_check)


def solution(mesh):
    torus = Mesh(
        mesh.devices.reshape(mesh.shape["dp"], 2, 4, 2), ("dp", "tensor_0", "tensor_1", "tensor_2")
    )
    return jax.shard_map(
        on_device,
        mesh=torus,
        in_specs=(
            P(DP_TENSOR, None),
            P(DP_TENSOR, None),
            P("dp"),
            P("dp", TENSOR),
            P("dp", TENSOR),
            P(TENSOR, "dp"),
        ),
        out_specs=(P(TENSOR, "dp"), P(TENSOR)),
        check_vma=False,
    )
```

profile of v0, /device:TPU:0, one launch (start us, length us, event | category | flops | bytes accessed | tf_op | source)
XLA Modules:
  0.0 199.9 jit_solution(10740757617195257877)
XLA Ops:
  7.2 0.0 copy-start
  7.2 12.1 %all_to_all.69 = bf16[8,8,1024]{2,0,1:T(8,128)(2,1)S(1)} all-to-all(bf16[8,8,1024]{2,0,1:T(8,128)(2,1)} %bitcast.50), channel_id=1, replica_groups=mesh['dp'=8,'tensor_0'=2,'tensor_1'=4,'tensor_2'=2] {'dp'}, dimensions={1} | all-to-all | bytes 262144 | tf_op jit(solution)/shard_map/all_to_all | solution.py:71
  19.3 0.1 broadcast_in_dim.15
  19.4 23.2 %all_to_all.70 = bf16[8,64,1024]{2,1,0:T(8,128)(2,1)S(1)} all-to-all(bf16[8,64,1024]{2,1,0:T(8,128)(2,1)S(1)} %broadcast_in_dim.15), channel_id=1, replica_groups=mesh['dp'=8,'tensor_0'=2,'tensor_1'=4,'tensor_2'=2] {'tensor_0','tensor_1'}, dimensions={0} | all-to-all | bytes 2097152 | tf_op jit(solution)/shard_map/all_to_all | solution.py:14
  42.6 0.3 broadcast_in_dim.16
  42.9 5.4 %all_to_all.71 = bf16[2,8,64,1024]{3,2,1,0:T(8,128)(2,1)S(1)} all-to-all(bf16[2,8,64,1024]{3,2,1,0:T(8,128)(2,1)S(1)} %broadcast_in_dim.16), channel_id=1, replica_groups=mesh['dp'=8,'tensor_0'=2,'tensor_1'=4,'tensor_2'=2] {'tensor_2'}, dimensions={0} | all-to-all | bytes 4194304 | tf_op jit(solution)/shard_map/all_to_all | solution.py:14
  48.3 0.2 copy.30
  48.6 0.0 copy-start.4
  48.6 1.3 copy-done.1
  49.9 0.5 multiply_reduce_fusion
  50.4 0.1 broadcast_in_dim.17
  50.5 0.6 broadcast_in_dim.18
  51.1 3.3 %all-to-all-start.3 = ((f32[8,1,1024]{2,1,0:T(1,128)}), f32[8,1,1024]{2,1,0:T(1,128)S(1)}, u32[]{:S(2)}, u32[]{:S(2)}) async-start(f32[8,1,1024]{2,1,0:T(1,128)} %broadcast_in_dim.18), calls=%async_computation.3 | async-start | bytes 65536 | tf_op jit(solution)/shard_map/all_to_all | solution.py:14
  54.5 0.0 reduce-scatter.4.cloned.1.call-start
  54.6 3.2 %copy.31 = bf16[8,16,8,1024]{3,2,1,0:T(8,128)(2,1)} copy(bf16[8,16,8,1024]{3,2,0,1:T(8,128)(2,1)} %bitcast.41) | data formatting | bytes 4194304 | tf_op jit(solution)/shard_map/transpose | solution.py:75
  57.8 2.9 %all-to-all-done.3 = f32[8,1,1024]{2,1,0:T(1,128)S(1)} async-done(((f32[8,1,1024]{2,1,0:T(1,128)}), f32[8,1,1024]{2,1,0:T(1,128)S(1)}, u32[]{:S(2)}, u32[]{:S(2)}) %all-to-all-start.3) | async-done | bytes 32800 | tf_op jit(solution)/shard_map/all_to_all | solution.py:14
  60.7 4.6 %convolution_convert_fusion.1 = bf16[1024,896]{0,1:T(8,128)(2,1)S(1)} fusion(bf16[1024,896]{1,0:T(8,128)(2,1)} %param.10, bf16[1024,1024]{1,0:T(8,128)(2,1)} %bitcast.43, f32[1024]{0:T(1024)S(1)} %convert_element_type.42, f32[1024]{0:T(1024)S(1)} %add_rsqrt_fusion), kind=kOutput, calls=%fused_computation.6 | convolution fusion | flops 1884160000 | bytes 5775360 | tf_op jit(solution)/shard_map/dot_general | solution.py:83
  65.3 2.3 %convolution_convert_fusion.2 = bf16[1024,896]{0,1:T(8,128)(2,1)S(1)} fusion(bf16[1024,896]{1,0:T(8,128)(2,1)S(1)} %copy-done.5, bf16[1024,1024]{1,0:T(8,128)(2,1)S(1)} %bitcast.45, f32[1024]{0:T(1024)S(1)} %convert_element_type.42, f32[1024]{0:T(1024)S(1)} %add_rsqrt_fusion), kind=kOutput, calls=%fused_computation.7 | convolution fusion | flops 1884160000 | bytes 5775360 | tf_op jit(solution)/shard_map/dot_general | solution.py:82
  67.7 2.2 %pad_maximum_fusion = bf16[1024,1792]{0,1:T(8,128)(2,1)} fusion(bf16[1024,896]{0,1:T(8,128)(2,1)S(1)} %convolution_convert_fusion.1, bf16[1024,896]{0,1:T(8,128)(2,1)S(1)} %convolution_convert_fusion.2), kind=kLoop, calls=%fused_computation.2 | loop fusion | flops 7340032 | bytes 7340032 | tf_op jit(solution)/shard_map/concatenate | solution.py:85
  69.9 6.0 %copy.39 = bf16[1024,1792]{1,0:T(8,128)(2,1)} copy(bf16[1024,1792]{0,1:T(8,128)(2,1)} %pad_maximum_fusion) | data formatting | bytes 7340032
  75.9 0.0 reduce-scatter.4.cloned.1.call-update
  75.9 0.7 copy-done.3
  76.6 0.1 all_to_all.53
  76.7 0.7 reshape.51
  77.4 3.5 %all-to-all-start.4 = ((s32[16,1,224]{2,1,0:T(1,128)}), s32[16,1,224]{2,1,0:T(1,128)S(1)}, u32[]{:S(2)}, u32[]{:S(2)}) async-start(s32[16,1,224]{2,1,0:T(1,128)} %reshape.51), calls=%async_computation.4 | async-start | bytes 32768 | tf_op jit(solution)/shard_map/all_to_all | solution.py:65
  80.9 0.1 shift_right_arithmetic.26
  81.0 8.1 %all-to-all-done.4 = s32[16,1,224]{2,1,0:T(1,128)S(1)} async-done(((s32[16,1,224]{2,1,0:T(1,128)}), s32[16,1,224]{2,1,0:T(1,128)S(1)}, u32[]{:S(2)}, u32[]{:S(2)}) %all-to-all-start.4) | async-done | bytes 14368 | tf_op jit(solution)/shard_map/all_to_all | solution.py:65
  89.1 0.5 broadcast.25
  89.6 0.7 reduce.4
  90.3 0.1 reshape.52
  90.4 0.1 copy.35
  90.4 30.3 %reduce-scatter.4.cloned.1.call-done = bf16[128,1792]{1,0:T(8,128)(2,1)} async-done(((bf16[1024,1792]{1,0:T(8,128)(2,1)}), bf16[128,1792]{1,0:T(8,128)(2,1)}) %reduce-scatter.4.cloned.1.call-update) | async-done | bytes 458768
  120.8 1.3 copy.40
  122.0 0.1 convert_element_type.44
  122.1 0.2 fusion.1
  122.3 0.2 copy.36
  122.5 0.2 broadcast_in_dim.19
  122.7 24.7 %all_to_all.72 = bf16[8,128,896]{2,1,0:T(8,128)(2,1)S(1)} all-to-all(bf16[8,128,896]{2,1,0:T(8,128)(2,1)S(1)} %broadcast_in_dim.19), channel_id=1, replica_groups=mesh['dp'=8,'tensor_0'=2,'tensor_1'=4,'tensor_2'=2] {'dp'}, dimensions={0} | all-to-all | bytes 3670016 | tf_op jit(solution)/shard_map/all_to_all | solution.py:14
  147.5 2.3 %convolution_convert_fusion = bf16[1024,1024]{1,0:T(8,128)(2,1)S(1)} fusion(bf16[1024,896]{1,0:T(8,128)(2,1)S(1)} %bitcast.47, bf16[896,1024]{1,0:T(8,128)(2,1)S(1)} %copy-done), kind=kOutput, calls=%fused_computation.5 | convolution fusion | flops 1880096768 | bytes 5767168 | tf_op jit(solution)/shard_map/dot_general | solution.py:93
  149.8 0.2 copy.44
  150.1 6.3 %all_to_all.73 = bf16[2,8,64,1024]{3,2,1,0:T(8,128)(2,1)} all-to-all(bf16[2,8,64,1024]{3,2,1,0:T(8,128)(2,1)S(1)} %bitcast.42), channel_id=1, replica_groups=mesh['dp'=8,'tensor_0'=2,'tensor_1'=4,'tensor_2'=2] {'tensor_2'}, dimensions={0} | all-to-all | bytes 4194304 | tf_op jit(solution)/shard_map/all_to_all | solution.py:48
  156.4 3.4 %reduce_sum.59 = bf16[8,64,1024]{2,1,0:T(8,128)(2,1)} reduce(bf16[2,8,64,1024]{3,2,1,0:T(8,128)(2,1)} %all_to_all.73, bf16[]{:T(256)} %constant.38.clone.1), dimensions={0}, to_apply=%region_3.4 | reduce | flops 524288 | bytes 3145730 | tf_op jit(solution)/shard_map/reduce_sum | solution.py:49
  159.7 6.5 %all-to-all-start.7 = ((bf16[8,64,1024]{2,1,0:T(8,128)(2,1)}), bf16[8,64,1024]{2,1,0:T(8,128)(2,1)S(1)}, u32[]{:S(2)}, u32[]{:S(2)}) async-start(bf16[8,64,1024]{2,1,0:T(8,128)(2,1)} %reduce_sum.59), calls=%async_computation.7 | async-start | bytes 2097152 | tf_op jit(solution)/shard_map/all_to_all | solution.py:56
  166.3 15.9 %all-to-all-done.7 = bf16[8,64,1024]{2,1,0:T(8,128)(2,1)S(1)} async-done(((bf16[8,64,1024]{2,1,0:T(8,128)(2,1)}), bf16[8,64,1024]{2,1,0:T(8,128)(2,1)S(1)}, u32[]{:S(2)}, u32[]{:S(2)}) %all-to-all-start.7) | async-done | bytes 1048608 | tf_op jit(solution)/shard_map/all_to_all | solution.py:56
  182.1 0.2 convert_reduce_fusion
  182.3 1.7 multiply_reduce_fusion.1
  184.0 8.5 %all_to_all.74 = f32[8,1,64]{2,1,0:T(1,128)S(1)} all-to-all(f32[8,1,64]{2,1,0:T(1,128)S(1)} %broadcast_in_dim.20), channel_id=1, replica_groups=mesh['dp'=8,'tensor_0'=2,'tensor_1'=4,'tensor_2'=2] {'dp'}, dimensions={0} | all-to-all | bytes 4096 | tf_op jit(solution)/shard_map/all_to_all | solution.py:14
  192.6 0.5 broadcast_multiply_fusion
  (17 shorter events, 0.1 us)
Async XLA Ops:
  7.2 140.3 %copy-start = (bf16[896,1024]{1,0:T(8,128)(2,1)S(1)}, bf16[896,1024]{1,0:T(8,128)(2,1)}, u32[]{:S(2)}) copy-start(bf16[896,1024]{1,0:T(8,128)(2,1)} %param.11) | copy-start | bytes 5505028
  48.6 1.4 copy-start.1
  48.6 6.0 %copy-start.4 = (bf16[1024]{0:T(1024)(128)(2,1)S(1)}, bf16[1024]{0:T(1024)(128)(2,1)}, u32[]{:S(2)}) copy-start(bf16[1024]{0:T(1024)(128)(2,1)} %param.8) | copy-start | bytes 6148
  51.1 9.5 %all-to-all-start.3 = ((f32[8,1,1024]{2,1,0:T(1,128)}), f32[8,1,1024]{2,1,0:T(1,128)S(1)}, u32[]{:S(2)}, u32[]{:S(2)}) async-start(f32[8,1,1024]{2,1,0:T(1,128)} %broadcast_in_dim.18), calls=%async_computation.3 | async-start | bytes 65536 | tf_op jit(solution)/shard_map/all_to_all | solution.py:14
  54.5 66.3 %reduce-scatter.4.cloned.1.call-start = ((), (), s32[]{:S(2)}) async-start(), calls=%async_computation.10 | async-start | bytes 4128768
  60.7 4.6 %copy-start.2 = (bf16[8,16,8,1024]{3,2,1,0:T(8,128)(2,1)S(1)}, bf16[8,16,8,1024]{3,2,1,0:T(8,128)(2,1)}, u32[]{:S(2)}) copy-start(bf16[8,16,8,1024]{3,2,1,0:T(8,128)(2,1)} %copy.31) | copy-start | bytes 6291460
  60.7 4.6 %copy-start.5 = (bf16[1024,896]{1,0:T(8,128)(2,1)S(1)}, bf16[1024,896]{1,0:T(8,128)(2,1)}, u32[]{:S(2)}) copy-start(bf16[1024,896]{1,0:T(8,128)(2,1)} %param.9) | copy-start | bytes 5505028
  75.9 0.7 copy-start.3
  77.4 11.6 %all-to-all-start.4 = ((s32[16,1,224]{2,1,0:T(1,128)}), s32[16,1,224]{2,1,0:T(1,128)S(1)}, u32[]{:S(2)}, u32[]{:S(2)}) async-start(s32[16,1,224]{2,1,0:T(1,128)} %reshape.51), calls=%async_computation.4 | async-start | bytes 32768 | tf_op jit(solution)/shard_map/all_to_all | solution.py:65
  159.7 22.4 %all-to-all-start.7 = ((bf16[8,64,1024]{2,1,0:T(8,128)(2,1)}), bf16[8,64,1024]{2,1,0:T(8,128)(2,1)S(1)}, u32[]{:S(2)}, u32[]{:S(2)}) async-start(bf16[8,64,1024]{2,1,0:T(8,128)(2,1)} %reduce_sum.59), calls=%async_computation.7 | async-start | bytes 2097152 | tf_op jit(solution)/shard_map/all_to_all | solution.py:56
Sparse Core Ops, SparseCore 0:
  76.0 44.6 reduce-scatter.3
where the time goes:
time: 201 us; the launch traced here: 200 us
  blocking collectives  80.4 us (40%)
  waiting for transfers between devices  57.2 us (28%)
  local copies, waits for them, and re-layouts  16 us (8%)
  between operations  14.3 us (7%)
  starting transfers between devices  13.4 us (7%)
  other arithmetic  9.45 us (5%)
  matrix products  9.26 us (5%)
    all_to_all x4, blocking collectives, sent_to_all(): lax.all_to_all(jnp.broadcast_to(value[None], (length, *value.shape)), axi...  61.9 us
    unnamed x2, waiting for transfers between devices  30.3 us
    all_to_all x1, waiting for transfers between devices, sum_in_two_steps(): lax.all_to_all(nearer.astype(jnp.bfloat16), far, split_axis=0, concat_axi...  15.9 us
    all_to_all x1, blocking collectives, on_device(): lax.all_to_all(saved_input, 'dp', split_axis=1, concat_axis=0, tiled=True)  12.1 us
    unnamed x16, local copies, waits for them, and re-layouts  10.1 us
    all_to_all x1, waiting for transfers between devices, on_device(): lax.all_to_all(keep_bits, TENSOR, split_axis=1, concat_axis=0, tiled=True)  8.05 us
    all_to_all x1, starting transfers between devices, sum_in_two_steps(): lax.all_to_all(nearer.astype(jnp.bfloat16), far, split_axis=0, concat_axi...  6.54 us
    all_to_all x1, blocking collectives, sum_at_owner(): lax.all_to_all(in_blocks(value, dim, length), axis, 0, 0, tiled=True)  6.31 us
  transfers between devices with their start and end apart: 4, of which 4 were waited for; matrix products, arithmetic and copies ran while one was open for 3% of the time, Pallas kernels for 0%

commit v1 on v0

v1 whole, which is shorter than its diff:
```python
import jax
import jax.numpy as jnp
from jax import lax
from jax.sharding import Mesh
from jax.sharding import PartitionSpec as P

D = 8192
DP = ("yl", "x")
TENSOR = ("yh", "z", "c")
CHIPS = ("yl", "x", "yh", "z")
SWAP = ((0, 1), (1, 0))


def split3(value):
    hi = value.astype(jnp.bfloat16)
    rest = value - hi.astype(jnp.float32)
    mid = rest.astype(jnp.bfloat16)
    low = (rest - mid.astype(jnp.float32)).astype(jnp.bfloat16)
    return hi, mid, low


def on_device(saved_input, keep_bits, norm_gain, gate_weight, up_weight, down_weight):
    core = lax.axis_index("c")
    rows = saved_input.shape[0]
    width = gate_weight.shape[0]
    units = gate_weight.shape[1]
    dp_width = lax.axis_size(DP)
    chip_tensor = lax.axis_size(("yh", "z"))

    wide = saved_input.astype(jnp.float32)
    inv_rms = lax.rsqrt(jnp.sum(wide * wide, axis=1, keepdims=True) / D + 1e-05)
    lane = lax.broadcasted_iota(jnp.int32, (rows, 128), 1)
    hi, mid, low = split3(inv_rms)
    zero = jnp.zeros((), jnp.bfloat16)
    extra = jnp.where(lane == 0, hi, jnp.where(lane == 1, mid, jnp.where(lane == 2, low, zero)))
    slices = saved_input.reshape(rows, dp_width, width).transpose(1, 0, 2)
    block = jnp.concatenate((slices, jnp.broadcast_to(extra[None], (dp_width, rows, 128))), axis=2)
    block = jnp.broadcast_to(block[:, None], (dp_width, chip_tensor, rows, width + 128))
    block = block.reshape(dp_width * chip_tensor, rows, width + 128)
    mine = lax.all_to_all(block, CHIPS, 0, 0, tiled=True)
    other = lax.ppermute(mine, "c", SWAP)

    gain = norm_gain.astype(jnp.float32)[None, :]

    def normed_of(part):
        part = part.reshape(-1, width + 128).astype(jnp.float32)
        scale = part[:, width : width + 1] + part[:, width + 1 : width + 2] + part[:, width + 2 : width + 3]
        return (part[:, :width] * scale * gain).astype(jnp.bfloat16)

    def projected(part):
        normed = normed_of(part)
        g = jnp.dot(normed, gate_weight, preferred_element_type=jnp.float32).astype(jnp.bfloat16)
        u = jnp.dot(normed, up_weight, preferred_element_type=jnp.float32).astype(jnp.bfloat16)
        return jnp.concatenate((g, u), axis=1).reshape(dp_width, -1, 2 * units)

    a, b = projected(mine), projected(other)
    first = jnp.where(core == 0, a, b)
    second = jnp.where(core == 0, b, a)
    partial = jnp.concatenate((first, second), axis=1)
    arrived = lax.all_to_all(partial, DP, 0, 0, tiled=True)
    summed = jnp.sum(arrived.astype(jnp.float32), axis=0)

    words = lax.all_to_all(keep_bits, TENSOR, split_axis=1, concat_axis=0, tiled=True)
    words = words.reshape(chip_tensor, 2, rows, -1).transpose(1, 0, 2, 3).reshape(2 * chip_tensor * rows, -1)
    shifts = jnp.arange(32, dtype=jnp.int32)
    keep = jnp.bitwise_and(jnp.right_shift(words[:, :, None], shifts[None, None, :]), 1)
    keep = 2.0 * keep.reshape(words.shape[0], -1).astype(jnp.float32)
    hidden = (jax.nn.silu(summed[:, :units]) * summed[:, units:] * keep).astype(jnp.bfloat16)

    per_dp = hidden.shape[0]
    hidden = jnp.broadcast_to(hidden[None], (dp_width, *hidden.shape))
    hidden = lax.all_to_all(hidden, DP, 0, 0, tiled=True).reshape(-1, units)
    out = jnp.dot(hidden, down_weight, preferred_element_type=jnp.float32)
    out = out.astype(jnp.bfloat16).reshape(dp_width, 2, 2, -1, rows, width)
    keep_half = lax.dynamic_index_in_dim(out, core, 2, keepdims=False)
    send_half = lax.dynamic_index_in_dim(out, 1 - core, 2, keepdims=False)
    came = lax.ppermute(send_half, "c", SWAP)
    half = (keep_half.astype(jnp.float32) + came.astype(jnp.float32)).astype(jnp.bfloat16)
    half = half.transpose(0, 2, 1, 3, 4).reshape(dp_width, -1, width)
    parts = lax.all_to_all(half, ("yh", "z"), 0, 0, tiled=True)
    mlp = jnp.sum(parts.astype(jnp.float32), axis=0)

    own = lax.axis_index(("yh", "z"))

    def raw_rows(part):
        part = part.reshape(dp_width, 2, -1, rows, width + 128)
        part = lax.dynamic_index_in_dim(part, own, 0, keepdims=False)
        part = lax.dynamic_index_in_dim(part, core, 0, keepdims=False)
        return part[:, :, :width]

    r_mine, r_other = raw_rows(mine), raw_rows(other)
    residual = jnp.stack(
        (jnp.where(core == 0, r_mine, r_other), jnp.where(core == 0, r_other, r_mine)), axis=1
    ).reshape(-1, width)
    layer_out = (residual.astype(jnp.float32) + mlp).astype(jnp.bfloat16)
    w = layer_out.astype(jnp.float32)
    squares = jnp.sum(w * w, axis=1)
    every = lax.all_to_all(jnp.broadcast_to(squares[None], (dp_width, squares.shape[0])), DP, 0, 0, tiled=True)
    return layer_out, jnp.sum(every, axis=0) / D


def solution(mesh):
    torus = Mesh(mesh.devices.reshape(2, 4, 2, 4, 2), ("yl", "x", "yh", "z", "c"))
    return jax.shard_map(
        on_device,
        mesh=torus,
        in_specs=(
            P(DP + TENSOR, None),
            P(DP + TENSOR, None),
            P(DP),
            P(DP, TENSOR),
            P(DP, TENSOR),
            P(TENSOR, DP),
        ),
        out_specs=(P(TENSOR, DP), P(TENSOR)),
        check_vma=False,
    )
```

time: 201 us -> 186 us (0.925)
  blocking collectives: 80.4 us -> 8.55 us
  waiting for transfers between devices: 57.2 us -> 101 us
  starting transfers between devices: 13.4 us -> 42.5 us
  between operations: 14.3 us -> 0.92 us
  local copies, waits for them, and re-layouts: 16 us -> 8.79 us
  other arithmetic: 9.45 us -> 13.7 us
    all_to_all x2 -> x4, waiting for transfers between devices: 18.8 us -> 98.7 us  [the longest x1 41.1 us: on_device(): arrived = lax.all_to_all(partial, DP, 0, 0, tiled=True)]
    all_to_all x6 -> x1, blocking collectives: 80.4 us -> 8.55 us  [on_device(): lax.all_to_all(jnp.broadcast_to(squares[None], (dp_width, squares.shape[0...]
    unnamed x2 -> x0, waiting for transfers between devices: 30.3 us -> none
    all_to_all x2 -> x4, starting transfers between devices: 9.88 us -> 37.9 us  [the longest x1 15.8 us: on_device(): hidden = lax.all_to_all(hidden, DP, 0, 0, tiled=True).reshape(-1, units)]
    all_to_all x1, waiting for transfers between devices: 8.05 us -> 0.01 us  [on_device(): lax.all_to_all(keep_bits, TENSOR, split_axis=1, concat_axis=0, tiled=True)]
    unnamed x16 -> x14, local copies, waits for them, and re-layouts: 10.1 us -> 2.13 us
    transpose x1, local copies, waits for them, and re-layouts: 3.22 us -> 0.01 us  [on_device(): words.reshape(chip_tensor, 2, rows, -1).transpose(1, 0, 2, 3)]
    ppermute x0 -> x2, waiting for transfers between devices: none -> 2.65 us  [the longest x1 2.65 us: on_device(): came = lax.ppermute(send_half, 'c', SWAP)]
  transfers between devices with their start and end apart: 4 -> 7, of which waited for: 4 -> 5; matrix products, arithmetic and copies ran while one was open for 3% -> 8% of each run, Pallas kernels for 0% -> 0%
where the time goes in v1:
time: 186 us; the launch traced here: 185 us
  waiting for transfers between devices  101 us (54%)
  starting transfers between devices  42.5 us (23%)
  other arithmetic  13.7 us (7%)
  matrix products  8.98 us (5%)
  local copies, waits for them, and re-layouts  8.79 us (5%)
  blocking collectives  8.55 us (5%)
    all_to_all x1, waiting for transfers between devices, on_device(): arrived = lax.all_to_all(partial, DP, 0, 0, tiled=True)  41.1 us
    all_to_all x1, waiting for transfers between devices, on_device(): hidden = lax.all_to_all(hidden, DP, 0, 0, tiled=True).reshape(-1, units)  23.9 us
    all_to_all x1, waiting for transfers between devices, on_device(): mine = lax.all_to_all(block, CHIPS, 0, 0, tiled=True)  18.7 us
    all_to_all x1, starting transfers between devices, on_device(): hidden = lax.all_to_all(hidden, DP, 0, 0, tiled=True).reshape(-1, units)  15.8 us
    all_to_all x1, waiting for transfers between devices, on_device(): parts = lax.all_to_all(half, ('yh', 'z'), 0, 0, tiled=True)  15 us
    all_to_all x1, starting transfers between devices, on_device(): mine = lax.all_to_all(block, CHIPS, 0, 0, tiled=True)  11.5 us
    all_to_all x1, blocking collectives, on_device(): lax.all_to_all(jnp.broadcast_to(squares[None], (dp_width, squares.shape[0...  8.55 us
    all_to_all x1, starting transfers between devices, on_device(): parts = lax.all_to_all(half, ('yh', 'z'), 0, 0, tiled=True)  6.15 us
  transfers between devices with their start and end apart: 7, of which 5 were waited for; matrix products, arithmetic and copies ran while one was open for 8% of the time, Pallas kernels for 0%

profile of v1, /device:TPU:0, one launch (start us, length us, event | category | flops | bytes accessed | tf_op | source)
XLA Modules:
  0.0 184.8 jit_solution(4852053231108895981)
XLA Ops:
  0.7 1.2 multiply_reduce_fusion.1
  1.9 0.1 select_select_fusion
  2.0 0.9 pad_maximum_fusion.3
  2.9 1.1 broadcast_in_dim.57
  4.0 11.5 %all-to-all-start = ((bf16[64,8,1152]{2,1,0:T(8,128)(2,1)}), bf16[64,8,1152]{2,1,0:T(8,128)(2,1)S(1)}, u32[]{:S(2)}, u32[]{:S(2)}) async-start(bf16[64,8,1152]{2,1,0:T(8,128)(2,1)} %bitcast.62), calls=%async_computation | async-start | bytes 2359296 | tf_op jit(solution)/shard_map/all_to_all | solution.py:40
  15.6 0.1 all_to_all.30
  15.7 0.7 reshape.197
  16.4 18.7 %all-to-all-done = bf16[64,8,1152]{2,1,0:T(8,128)(2,1)S(1)} async-done(((bf16[64,8,1152]{2,1,0:T(8,128)(2,1)}), bf16[64,8,1152]{2,1,0:T(8,128)(2,1)S(1)}, u32[]{:S(2)}, u32[]{:S(2)}) %all-to-all-start) | async-done | bytes 1179680 | tf_op jit(solution)/shard_map/all_to_all | solution.py:40
  35.1 4.0 %all-to-all-start.2 = ((s32[16,1,224]{2,1,0:T(1,128)}), s32[16,1,224]{2,1,0:T(1,128)S(1)}, u32[]{:S(2)}, u32[]{:S(2)}) async-start(s32[16,1,224]{2,1,0:T(1,128)} %reshape.197), calls=%async_computation.2 | async-start | bytes 32768 | tf_op jit(solution)/shard_map/all_to_all | solution.py:63
  39.1 0.5 collective-permute-start
  39.5 0.2 bitcast_convert_fusion.1
  39.7 0.3 fusion.8
  40.0 0.5 copy-done.4
  40.6 1.3 convolution_convert_fusion.3
  41.9 0.2 copy-done.5
  42.1 1.3 convolution_convert_fusion.4
  43.4 0.2 bitcast_convert_fusion
  43.5 0.3 fusion.7
  43.8 0.6 copy-done.1
  44.4 1.3 convolution_convert_fusion.1
  45.7 1.3 convolution_convert_fusion.2
  47.0 0.7 broadcast_select_fusion.1
  47.7 2.1 %pad_maximum_fusion = bf16[8,128,1792]{2,1,0:T(8,128)(2,1)} fusion(bf16[8,64,1792]{2,1,0:T(8,128)(2,1)S(1)} %bitcast.60, bf16[8,64,1792]{2,1,0:T(8,128)(2,1)S(1)} %bitcast.59), kind=kLoop, calls=%fused_computation.1 | loop fusion | flops 7340032 | bytes 7340032 | tf_op jit(solution)/shard_map/concatenate | solution.py:59
  49.8 4.5 %all-to-all-start.1 = ((bf16[8,128,1792]{2,1,0:T(8,128)(2,1)}), bf16[8,128,1792]{2,1,0:T(8,128)(2,1)}, u32[]{:S(2)}, u32[]{:S(2)}) async-start(bf16[8,128,1792]{2,1,0:T(8,128)(2,1)} %pad_maximum_fusion), calls=%async_computation.1 | async-start | bytes 7340032 | tf_op jit(solution)/shard_map/all_to_all | solution.py:60
  54.3 0.1 shift_right_arithmetic.26
  54.4 0.5 broadcast.132
  54.9 0.7 reduce.9
  55.6 0.1 reshape.198
  55.8 0.9 shift_right_arithmetic.23
  56.6 1.2 copy.48
  57.8 41.1 %all-to-all-done.1 = bf16[8,128,1792]{2,1,0:T(8,128)(2,1)} async-done(((bf16[8,128,1792]{2,1,0:T(8,128)(2,1)}), bf16[8,128,1792]{2,1,0:T(8,128)(2,1)}, u32[]{:S(2)}, u32[]{:S(2)}) %all-to-all-start.1) | async-done | bytes 3670048 | tf_op jit(solution)/shard_map/all_to_all | solution.py:60
  99.0 2.6 %convert_reduce_fusion = f32[128,1792]{1,0:T(8,128)S(1)} fusion(bf16[8,128,1792]{2,1,0:T(8,128)(2,1)} %all-to-all-done.1), kind=kLoop, calls=%fused_computation | loop fusion | flops 3440640 | bytes 4587520 | tf_op jit(solution)/shard_map/reduce_sum | solution.py:61
  101.6 0.2 fusion.6
  101.8 1.5 broadcast_in_dim.58
  103.3 15.8 %all-to-all-start.3 = ((bf16[8,128,896]{2,1,0:T(8,128)(2,1)}), bf16[8,128,896]{2,1,0:T(8,128)(2,1)}, u32[]{:S(2)}, u32[]{:S(2)}) async-start(bf16[8,128,896]{2,1,0:T(8,128)(2,1)} %broadcast_in_dim.58), calls=%async_computation.3 | async-start | bytes 3670016 | tf_op jit(solution)/shard_map/all_to_all | solution.py:72
  119.0 23.9 %all-to-all-done.3 = bf16[8,128,896]{2,1,0:T(8,128)(2,1)} async-done(((bf16[8,128,896]{2,1,0:T(8,128)(2,1)}), bf16[8,128,896]{2,1,0:T(8,128)(2,1)}, u32[]{:S(2)}, u32[]{:S(2)}) %all-to-all-start.3) | async-done | bytes 1835040 | tf_op jit(solution)/shard_map/all_to_all | solution.py:72
  143.0 3.8 %convolution_convert_fusion = bf16[1024,1024]{1,0:T(8,128)(2,1)S(1)} fusion(bf16[1024,896]{1,0:T(8,128)(2,1)} %bitcast.22, bf16[896,1024]{1,0:T(8,128)(2,1)S(1)} %copy-done), kind=kOutput, calls=%fused_computation.11 | convolution fusion | flops 1880096768 | bytes 5767168 | tf_op jit(solution)/shard_map/dot_general | solution.py:73
  146.8 0.3 constant_dynamic-slice_fusion.1
  147.2 0.1 collective-permute-start.1
  147.2 2.6 %collective-permute-done.1 = bf16[8,2,4,8,1024]{4,3,1,2,0:T(8,128)(2,1)S(1)} collective-permute-done((bf16[8,2,4,8,1024]{4,3,1,2,0:T(8,128)(2,1)S(1)}, bf16[8,2,4,8,1024]{4,3,1,2,0:T(8,128)(2,1)S(1)}, u32[]{:S(2)}, u32[]{:S(2)}) %collective-permute-start.1) | collective-permute-done | bytes 1048608 | tf_op jit(solution)/shard_map/ppermute | solution.py:77
  149.9 1.4 fusion.4
  151.3 6.2 %all-to-all-start.4 = ((bf16[8,64,1024]{2,1,0:T(8,128)(2,1)}), bf16[8,64,1024]{2,1,0:T(8,128)(2,1)}, u32[]{:S(2)}, u32[]{:S(2)}) async-start(bf16[8,64,1024]{2,1,0:T(8,128)(2,1)} %bitcast.63), calls=%async_computation.4 | async-start | bytes 2097152 | tf_op jit(solution)/shard_map/all_to_all | solution.py:80
  157.5 0.9 dynamic-slice_bitcast_fusion
  158.4 15.0 %all-to-all-done.4 = bf16[8,64,1024]{2,1,0:T(8,128)(2,1)} async-done(((bf16[8,64,1024]{2,1,0:T(8,128)(2,1)}), bf16[8,64,1024]{2,1,0:T(8,128)(2,1)}, u32[]{:S(2)}, u32[]{:S(2)}) %all-to-all-start.4) | async-done | bytes 1048608 | tf_op jit(solution)/shard_map/all_to_all | solution.py:80
  173.4 1.4 convert_reduce_fusion.1
  174.9 0.8 multiply_reduce_fusion
  175.7 8.5 %all_to_all.42 = f32[8,1,64]{2,1,0:T(1,128)S(1)} all-to-all(f32[8,1,64]{2,1,0:T(1,128)S(1)} %broadcast_in_dim.59), channel_id=1, replica_groups=mesh['yl'=2,'x'=4,'yh'=2,'z'=4,'c'=2] {'yl','x'}, dimensions={0} | all-to-all | bytes 4096 | tf_op jit(solution)/shard_map/all_to_all | solution.py:98
  184.3 0.5 broadcast_multiply_fusion
  (26 shorter events, 0.3 us)
Async XLA Ops:
  0.6 142.3 %copy-start = (bf16[896,1024]{1,0:T(8,128)(2,1)S(1)}, bf16[896,1024]{1,0:T(8,128)(2,1)}, u32[]{:S(2)}) copy-start(bf16[896,1024]{1,0:T(8,128)(2,1)} %param.11) | copy-start | bytes 5505028
  0.6 14.9 %copy-start.3 = (bf16[1024]{0:T(1024)(128)(2,1)S(1)}, bf16[1024]{0:T(1024)(128)(2,1)}, u32[]{:S(2)}) copy-start(bf16[1024]{0:T(1024)(128)(2,1)} %param.8) | copy-start | bytes 6148
  0.7 14.9 %copy-start.2 = (s32[8,448]{1,0:T(8,128)S(1)}, s32[8,448]{1,0:T(8,128)}, u32[]{:S(2)}) copy-start(s32[8,448]{1,0:T(8,128)} %param.7) | copy-start | bytes 43012
  4.0 31.1 %all-to-all-start = ((bf16[64,8,1152]{2,1,0:T(8,128)(2,1)}), bf16[64,8,1152]{2,1,0:T(8,128)(2,1)S(1)}, u32[]{:S(2)}, u32[]{:S(2)}) async-start(bf16[64,8,1152]{2,1,0:T(8,128)(2,1)} %bitcast.62), calls=%async_computation | async-start | bytes 2359296 | tf_op jit(solution)/shard_map/all_to_all | solution.py:40
  35.1 14.7 %all-to-all-start.2 = ((s32[16,1,224]{2,1,0:T(1,128)}), s32[16,1,224]{2,1,0:T(1,128)S(1)}, u32[]{:S(2)}, u32[]{:S(2)}) async-start(s32[16,1,224]{2,1,0:T(1,128)} %reshape.197), calls=%async_computation.2 | async-start | bytes 32768 | tf_op jit(solution)/shard_map/all_to_all | solution.py:63
  39.1 1.5 copy-start.4
  39.1 4.3 %collective-permute-start = (bf16[64,8,1152]{2,1,0:T(8,128)(2,1)S(1)}, bf16[64,8,1152]{2,1,0:T(8,128)(2,1)S(1)}, u32[]{:S(2)}, u32[]{:S(2)}) collective-permute-start(bf16[64,8,1152]{2,1,0:T(8,128)(2,1)S(1)} %all-to-all-done), channel_id=1, source_target_pairs={{0,1},{1,0},{2,3},{3,2},{4,5},{5,4},{6,7},{7,6},{8,9},{9,8},{10,11... | collective-permute-start | bytes 3538952 | tf_op jit(solution)/shard_map/ppermute | solution.py:41
  40.6 1.5 copy-start.5
  43.4 1.1 copy-start.1
  49.8 49.2 %all-to-all-start.1 = ((bf16[8,128,1792]{2,1,0:T(8,128)(2,1)}), bf16[8,128,1792]{2,1,0:T(8,128)(2,1)}, u32[]{:S(2)}, u32[]{:S(2)}) async-start(bf16[8,128,1792]{2,1,0:T(8,128)(2,1)} %pad_maximum_fusion), calls=%async_computation.1 | async-start | bytes 7340032 | tf_op jit(solution)/shard_map/all_to_all | solution.py:60
  103.3 39.7 %all-to-all-start.3 = ((bf16[8,128,896]{2,1,0:T(8,128)(2,1)}), bf16[8,128,896]{2,1,0:T(8,128)(2,1)}, u32[]{:S(2)}, u32[]{:S(2)}) async-start(bf16[8,128,896]{2,1,0:T(8,128)(2,1)} %broadcast_in_dim.58), calls=%async_computation.3 | async-start | bytes 3670016 | tf_op jit(solution)/shard_map/all_to_all | solution.py:72
  147.2 2.7 %collective-permute-start.1 = (bf16[8,2,4,8,1024]{4,3,1,2,0:T(8,128)(2,1)S(1)}, bf16[8,2,4,8,1024]{4,3,1,2,0:T(8,128)(2,1)S(1)}, u32[]{:S(2)}, u32[]{:S(2)}) collective-permute-start(bf16[8,2,4,8,1024]{4,3,1,2,0:T(8,128)(2,1)S(1)} %bitcast.67), channel_id=1, source_target_pairs={{0,1},{1,0},{2,3},{3,2},{4,5},{5,4},{6,7},{7,6},{8,9},{9,8},{10,11... | collective-permute-start | bytes 3145736 | tf_op jit(solution)/shard_map/ppermute | solution.py:77
  151.3 22.1 %all-to-all-start.4 = ((bf16[8,64,1024]{2,1,0:T(8,128)(2,1)}), bf16[8,64,1024]{2,1,0:T(8,128)(2,1)}, u32[]{:S(2)}, u32[]{:S(2)}) async-start(bf16[8,64,1024]{2,1,0:T(8,128)(2,1)} %bitcast.63), calls=%async_computation.4 | async-start | bytes 2097152 | tf_op jit(solution)/shard_map/all_to_all | solution.py:80
